TPU v7x, 32 devices: a whole 2x2x4 slice. The times are simulated.
32 devices in a mesh: freq: 4 (over y, core), stn: 8 (over z, x).
Axes of the slice: x: 2, y: 2, z: 4, core: 2. Of those that a mesh axis runs over, the one named last changes fastest.
Arguments:
- samples: bfloat16 [4, 256, 24, 2, 128], P('freq', 'stn'), may hold values from -8 to 8, as said below
- window: float32 [128], replicated, may hold values from 0.1 to 1
- group_of_device: int32 [8], replicated, may hold values from 0 to 7, each once
- owner_map: int32 [8, 8], replicated, may hold values from 0 to 7, as said below
Outputs:
- owned: bfloat16 [2, 32, 8, 8, 1024], P(None, None, 'stn', 'freq')
Inputs may be any that keep to these rules, and one draw needn't show every extreme that they name: `samples`: samples are finite and bounded. Every row and every column of owner_map names each stn index exactly once.
All inputs are finite; a program needn't handle non-finite values.
Results may differ from a plain program's by a relative error of at most 0.0065.
Values may be sent and summed in bfloat16 or wider, within the bound.
A program may use at most 64 MiB of HBM per device.

v0:
```python
import math

import jax
import jax.numpy as jnp
from jax import lax
from jax.sharding import PartitionSpec as P

FFT_LEN = 128
AVG = 16
SPEC = 24
CH_OUT = 8


def channel_matrix(window):
    length = window.shape[0]
    index = jnp.arange(length, dtype=jnp.int32)
    product = index[:, None] * index[None, :] % length
    theta = product.astype(jnp.float32) * (2.0 * math.pi / length)
    weights = window[:, None] / math.sqrt(length)
    cosine = weights * jnp.cos(theta)
    sine = weights * jnp.sin(theta)
    upper = jnp.concatenate([cosine, -sine], axis=1)
    lower = jnp.concatenate([sine, cosine], axis=1)
    return jnp.concatenate([upper, lower], axis=0)


def split_matrix(matrix):
    high = matrix.astype(jnp.bfloat16)
    low = (matrix - high.astype(jnp.float32)).astype(jnp.bfloat16)
    return (high, low)


def channelize(block, high, low):
    rows = block.shape[0]
    flat = block.reshape(rows * SPEC, 2 * FFT_LEN)
    spectra = jnp.dot(flat, high, preferred_element_type=jnp.float32) + jnp.dot(
        flat, low, preferred_element_type=jnp.float32
    )
    spectra = spectra.astype(jnp.bfloat16).reshape(rows, SPEC, 2, CH_OUT, AVG)
    return spectra.transpose(3, 0, 2, 1, 4).reshape(CH_OUT, rows, 2 * SPEC * AVG)


def with_swapped(spectra):
    half = spectra.shape[2] // 2
    return jnp.stack(
        [spectra, jnp.concatenate([spectra[..., half:], -spectra[..., :half]], axis=-1)]
    )


def correlate(stacked, remote):
    block = jnp.einsum("pcak,cbk->pcab", stacked, remote, preferred_element_type=jnp.float32)
    return (block * (1.0 / (AVG * SPEC))).astype(jnp.bfloat16)


def channel_plan(local, group_of_device, owner_map, device_of_group, here, groups):
    rows_in = local.shape[1]
    spread = groups // CH_OUT
    quarter = here % spread
    copies = jnp.repeat(local, spread, axis=0)
    turned = lax.all_to_all(copies, "stn", split_axis=0, concat_axis=1, tiled=True)
    span = CH_OUT * rows_in
    mine = lax.dynamic_slice_in_dim(turned, quarter * span, span, 1)
    block = correlate(with_swapped(mine), turned)
    order = jnp.arange(groups, dtype=jnp.int32)
    column_for = (
        jnp.zeros((groups, groups), jnp.int32)
        .at[order[:, None], owner_map]
        .set(jnp.broadcast_to(order[None, :], (groups, groups)))
    )
    row_source = quarter * CH_OUT + jnp.arange(CH_OUT, dtype=jnp.int32)
    row_group = group_of_device[row_source]
    column_device = device_of_group[column_for[row_group]]
    vis = block.reshape(2, CH_OUT, rows_in, groups, rows_in).transpose(0, 1, 3, 2, 4)
    picked = jnp.take_along_axis(vis, column_device[None, :, :, None, None], axis=2)
    outgoing = picked.reshape(2, CH_OUT, groups, rows_in * rows_in)
    received = lax.all_to_all(outgoing, "stn", split_axis=2, concat_axis=2, tiled=True)
    arranged = received.reshape(2, CH_OUT, CH_OUT, spread, rows_in * rows_in).transpose(
        0, 2, 3, 1, 4
    )
    arranged = arranged.reshape(2, CH_OUT, groups, rows_in * rows_in)
    return jnp.take(arranged, device_of_group, axis=2)


def shards(samples, window, group_of_device, owner_map):
    groups = lax.axis_size("stn")
    here = lax.axis_index("stn")
    high, low = split_matrix(channel_matrix(window))
    local = channelize(samples[0], high, low)
    order = jnp.arange(groups, dtype=jnp.int32)
    device_of_group = jnp.zeros((groups,), jnp.int32).at[group_of_device].set(order)
    by_group = channel_plan(local, group_of_device, owner_map, device_of_group, here, groups)
    regrouped = lax.all_to_all(by_group, "freq", split_axis=2, concat_axis=1, tiled=True)
    return regrouped[:, :, None]


def solution(mesh):
    return jax.shard_map(
        shards,
        mesh=mesh,
        in_specs=(P("freq", "stn", None, None, None), P(), P(), P()),
        out_specs=P(None, None, "stn", "freq", None),
        check_vma=False,
    )
```

profile of v0, /device:TPU:0, one launch (start us, length us, event | category | flops | bytes accessed | tf_op | source)
XLA Modules:
  0.0 58.0 jit_solution(11295048349949106297)
XLA Ops:
  0.0 0.7 %broadcast_multiply_fusion = f32[128]{0:T(128)S(1)} fusion(f32[128]{0:T(128)} %param.5), kind=kLoop, calls=%fused_computation.69 | loop fusion | flops 128 | bytes 1024 | tf_op jit(solution)/shard_map/div | solution.py:19
  0.7 0.3 fusion.20
  1.0 1.3 %fusion.7 = f32[256,768]{1,0:T(8,128)S(1)} fusion(bf16[96,8,2,128]{3,2,1,0:T(2,128)(2,1)} %bitcast.75, f32[128,128]{1,0:T(8,128)S(1)} %get-tuple-element.9, f32[128,128]{1,0:T(8,128)S(1)} %get-tuple-element.8, f32[128,128]{1,0:T(8,128)S(1)} %get-tuple-element.7), kind=kOutput, calls=%fused_computation.18 | convolution fusion | flops 101187584 | bytes 1376256 | tf_op jit(solution)/shard_map/dot_general | solution.py:36
  2.3 0.3 fusion.2
  2.6 3.4 %reshape.92 = bf16[32,24,2,8,16]{1,0,4,3,2:T(8,128)(2,1)S(1)} reshape(bf16[768,256]{0,1:T(8,128)(2,1)S(1)} %fusion.2) | data formatting | bytes 786432 | tf_op jit(solution)/shard_map/reshape | solution.py:39
  6.1 2.9 %copy.28 = bf16[8,32,2,24,16]{1,4,3,2,0:T(8,128)(2,1)} copy(bf16[8,32,2,24,16]{3,1,4,0,2:T(8,128)(2,1)S(1)} %bitcast.70) | data formatting | bytes 786432 | tf_op jit(solution)/shard_map/transpose | solution.py:40
  8.9 2.3 %copy.29 = bf16[8,32,768]{2,1,0:T(8,128)(2,1)} copy(bf16[8,32,768]{1,2,0:T(8,128)(2,1)} %bitcast.71) | data formatting | bytes 786432 | tf_op jit(solution)/shard_map/reshape;broadcast_in_dim;reshape | solution.py:59
  11.3 7.3 %all-to-all-start = ((bf16[8,32,768]{2,1,0:T(8,128)(2,1)}), bf16[8,32,768]{2,1,0:T(8,128)(2,1)S(1)}, u32[]{:S(2)}, u32[]{:S(2)}) async-start(bf16[8,32,768]{2,1,0:T(8,128)(2,1)} %copy.29), calls=%async_computation | async-start | bytes 786432 | tf_op jit(solution)/shard_map/all_to_all | solution.py:60
  18.7 0.1 reshape.146
  18.8 0.6 %gather_fusion = s32[8]{0:T(128)S(1)} fusion(s32[8]{0:T(128)S(1)} %copy-done, s32[1024]{0:T(1024)S(1)} %pad_clamp_fusion.3), kind=kCustom, calls=%fused_computation | custom fusion | bytes 96 | tf_op jit(solution)/shard_map/gather | solution.py:71
  19.5 3.5 %scatter_fusion = s32[8,8]{1,0:T(8,128)S(1)} fusion(s32[8,8]{1,0:T(8,128)S(1)} %broadcast.121, s32[64]{0:T(128)S(1)} %reshape.144, s32[64]{0:T(128)S(1)} %reshape.146), kind=kCustom, calls=%fused_computation.6 | custom fusion | bytes 1280 | tf_op jit(solution)/shard_map/scatter | solution.py:68
  22.9 0.6 gather_fusion.1
  23.6 0.6 %scatter_custom_fusion = s32[8]{0:T(128)S(1)} fusion(s32[8]{0:T(128)S(1)} %compare_select_fusion.6, s32[8]{0:T(128)S(1)} %iota.20, s32[]{:T(128)} %constant.43.clone.1), kind=kCustom, calls=%fused_computation.70 | custom fusion | bytes 36 | tf_op jit(solution)/shard_map/scatter | solution.py:90
  24.2 0.8 %gather_fusion.2 = s32[64]{0:T(128)S(1)} fusion(s32[8]{0:T(128)S(1)} %scatter_custom_fusion, s32[1024]{0:T(1024)S(1)} %pad_clamp_fusion.1), kind=kCustom, calls=%fused_computation.2 | custom fusion | bytes 768 | tf_op jit(solution)/shard_map/gather | solution.py:72
  25.0 0.1 gather.30
  25.2 0.1 reshape.130
  25.3 5.0 %all-to-all-done = bf16[8,32,768]{2,1,0:T(8,128)(2,1)S(1)} async-done(((bf16[8,32,768]{2,1,0:T(8,128)(2,1)}), bf16[8,32,768]{2,1,0:T(8,128)(2,1)S(1)}, u32[]{:S(2)}, u32[]{:S(2)}) %all-to-all-start) | async-done | bytes 393248 | tf_op jit(solution)/shard_map/all_to_all | solution.py:60
  30.3 0.4 fusion.3
  30.7 0.4 reshape.95
  31.2 0.9 %copy.30 = bf16[2,8,32,8,32]{4,2,3,1,0:T(8,128)(2,1)S(1)} copy(bf16[2,8,32,8,32]{2,1,4,3,0:T(8,128)(2,1)S(1)} %reshape.95) | data formatting | bytes 524288 | tf_op jit(solution)/shard_map/reshape | solution.py:73
  32.1 0.8 %gather_fusion.4 = bf16[64,2,32,32]{3,2,1,0:T(8,128)(2,1)S(1)} fusion(bf16[2,8,8,32,32]{4,3,2,1,0:T(8,128)(2,1)S(1)} %bitcast.73, s32[64]{0:T(128)S(1)} %reshape.130), kind=kCustom, calls=%fused_computation.4 | custom fusion | bytes 524800 | tf_op jit(solution)/shard_map/jit(take_along_axis)/gather | solution.py:74
  32.9 0.1 copy.50
  33.0 1.2 %gather.32 = bf16[2,8,8,1024]{3,2,1,0:T(8,128)(2,1)S(1)} reshape(bf16[2,8,8,32,32]{4,3,2,1,0:T(8,128)(2,1)S(1)} %bitcast.72) | data formatting | bytes 524288 | tf_op jit(solution)/shard_map/jit(take_along_axis)/gather | solution.py:74
  34.1 0.1 broadcast_select_fusion
  34.2 0.9 %copy.32 = bf16[2,8,8,1024]{3,1,0,2:T(8,128)(2,1)} copy(bf16[2,8,8,1024]{3,2,1,0:T(8,128)(2,1)S(1)} %broadcast_select_fusion) | data formatting | bytes 524288 | tf_op jit(solution)/shard_map/jit(take_along_axis)/select_n | solution.py:74
  35.1 3.6 %all-to-all-start.1 = ((bf16[2,8,8,1024]{3,1,0,2:T(8,128)(2,1)}), bf16[2,8,8,1024]{3,1,0,2:T(8,128)(2,1)S(1)}, u32[]{:S(2)}, u32[]{:S(2)}) async-start(bf16[2,8,8,1024]{3,1,0,2:T(8,128)(2,1)} %copy.32), calls=%async_computation.1 | async-start | bytes 524288 | tf_op jit(solution)/shard_map/all_to_all | solution.py:76
  38.8 8.8 %all-to-all-done.1 = bf16[2,8,8,1024]{3,1,0,2:T(8,128)(2,1)S(1)} async-done(((bf16[2,8,8,1024]{3,1,0,2:T(8,128)(2,1)}), bf16[2,8,8,1024]{3,1,0,2:T(8,128)(2,1)S(1)}, u32[]{:S(2)}, u32[]{:S(2)}) %all-to-all-start.1) | async-done | bytes 262176 | tf_op jit(solution)/shard_map/all_to_all | solution.py:76
  47.6 0.1 copy.52
  47.7 0.6 gather_fusion.3
  48.3 0.1 select_bitcast_fusion
  48.4 8.6 %all_to_all.32 = bf16[2,8,8,1024]{3,1,0,2:T(8,128)(2,1)S(1)} all-to-all(bf16[2,8,8,1024]{3,1,0,2:T(8,128)(2,1)S(1)} %select_bitcast_fusion), channel_id=1, replica_groups=mesh['freq'=4,'stn'=8] {'freq'}, dimensions={2} | all-to-all | bytes 524288 | tf_op jit(solution)/shard_map/all_to_all | solution.py:92
  57.0 1.0 %copy.36 = bf16[2,32,1,2,1024]{4,3,2,1,0:T(2,128)(2,1)} copy(bf16[2,32,1,2,1024]{4,1,3,0,2:T(8,128)(2,1)S(1)} %bitcast.82) | data formatting | bytes 524288 | tf_op jit(solution)/shard_map/broadcast_in_dim | solution.py:93
  (28 shorter events, 0.4 us)
Async XLA Ops:
  0.0 2.3 %copy-start.1 = (bf16[1,32,24,2,128]{4,3,2,1,0:T(2,128)(2,1)S(1)}, bf16[1,32,24,2,128]{4,3,2,1,0:T(2,128)(2,1)}, u32[]{:S(2)}) copy-start(bf16[1,32,24,2,128]{4,3,2,1,0:T(2,128)(2,1)} %param.4) | copy-start | bytes 1179652
  8.9 9.6 %copy-start.2 = (s32[8,8]{1,0:T(8,128)S(1)}, s32[8,8]{1,0:T(8,128)}, u32[]{:S(2)}) copy-start(s32[8,8]{1,0:T(8,128)} %param.7) | copy-start | bytes 772
  8.9 9.8 %copy-start = (s32[8]{0:T(128)S(1)}, s32[8]{0:T(128)}, u32[]{:S(2)}) copy-start(s32[8]{0:T(128)} %param.6) | copy-start | bytes 100
  11.3 19.0 %all-to-all-start = ((bf16[8,32,768]{2,1,0:T(8,128)(2,1)}), bf16[8,32,768]{2,1,0:T(8,128)(2,1)S(1)}, u32[]{:S(2)}, u32[]{:S(2)}) async-start(bf16[8,32,768]{2,1,0:T(8,128)(2,1)} %copy.29), calls=%async_computation | async-start | bytes 786432 | tf_op jit(solution)/shard_map/all_to_all | solution.py:60
  35.1 12.5 %all-to-all-start.1 = ((bf16[2,8,8,1024]{3,1,0,2:T(8,128)(2,1)}), bf16[2,8,8,1024]{3,1,0,2:T(8,128)(2,1)S(1)}, u32[]{:S(2)}, u32[]{:S(2)}) async-start(bf16[2,8,8,1024]{3,1,0,2:T(8,128)(2,1)} %copy.32), calls=%async_computation.1 | async-start | bytes 524288 | tf_op jit(solution)/shard_map/all_to_all | solution.py:76
where the time goes:
time: 58.4 us; the launch traced here: 58 us
  local copies, waits for them, and re-layouts  21.1 us (36%)
  waiting for transfers between devices  13.8 us (24%)
  starting transfers between devices  10.9 us (19%)
  blocking collectives  8.59 us (15%)
  matrix products  2.02 us (3%)
  other arithmetic  1.33 us (2%)
    all_to_all x1, waiting for transfers between devices, channel_plan(): lax.all_to_all(outgoing, 'stn', split_axis=2, concat_axis=2, tiled=True)  8.8 us
    all_to_all x1, blocking collectives, shards(): lax.all_to_all(by_group, 'freq', split_axis=2, concat_axis=1, tiled=True)  8.59 us
    all_to_all x1, starting transfers between devices, channel_plan(): lax.all_to_all(copies, 'stn', split_axis=0, concat_axis=1, tiled=True)  7.28 us
    all_to_all x1, waiting for transfers between devices, channel_plan(): lax.all_to_all(copies, 'stn', split_axis=0, concat_axis=1, tiled=True)  5 us
    all_to_all x1, starting transfers between devices, channel_plan(): lax.all_to_all(outgoing, 'stn', split_axis=2, concat_axis=2, tiled=True)  3.64 us
    scatter x1, local copies, waits for them, and re-layouts, channel_plan(): column_for = jnp.zeros((groups, groups), jnp.int32).at[order[:, None], ow...  3.45 us
    reshape x1, local copies, waits for them, and re-layouts, channelize(): spectra = spectra.astype(jnp.bfloat16).reshape(rows, SPEC, 2, CH_OUT, AVG)  3.43 us
    transpose x1, local copies, waits for them, and re-layouts, channelize(): spectra.transpose(3, 0, 2, 1, 4).reshape(CH_OUT, rows, 2 * SPEC * AVG)  2.86 us
  transfers between devices with their start and end apart: 2, of which 2 were waited for; matrix products, arithmetic and copies ran while one was open for 11% of the time, Pallas kernels for 0%

commit v1 on v0

v1 whole, which is shorter than its diff:
```python
import functools
import math

import jax
import jax.numpy as jnp
import numpy as np
from jax import lax
from jax.experimental import pallas as pl
from jax.experimental.pallas import tpu as pltpu
from jax.sharding import PartitionSpec as P

AVG = 16
LANES = 128
MESH = pl.DeviceIdType.MESH


def swap_blocks(blocks, width):
    blocks = list(blocks)
    count = len(blocks)
    lane = lax.broadcasted_iota(jnp.int32, blocks[0].shape, 1) // width
    step = count // 2
    while step:
        upper = (lane // step) % 2 == 1
        for i in range(count):
            if (i // step) % 2 == 0:
                u, v = blocks[i], blocks[i + step]
                shift = step * width
                blocks[i] = jnp.where(upper, pltpu.roll(v, shift, 1), u)
                blocks[i + step] = jnp.where(upper, v, pltpu.roll(u, LANES - shift, 1))
        step //= 2
    return blocks


def kernel(
    nf, ns, rows, spec,
    x_ref, w_ref, cos_ref, sin_ref, god_ref, own_ref,
    out_ref,
    xf, send1, held, left, vis, tiles, mixed, send2, dev_of, table,
    ssem1, rsem1, ssem2, rsem2,
):
    length = LANES
    ch_out = length // AVG
    spread = ns // ch_out
    rpf = ns // nf
    fl_count = ch_out // rpf
    half = spec * AVG
    b = lax.axis_index("freq")
    me = lax.axis_index("stn")
    total = nf * ns
    rank = b * ns + me

    barrier = pltpu.get_barrier_semaphore()

    def greet(off, carry):
        other = lax.rem(rank + off, total)
        pl.semaphore_signal(
            barrier, inc=1, device_id=(other // ns, lax.rem(other, ns)), device_id_type=MESH
        )
        return carry

    lax.fori_loop(1, total, greet, 0)

    weights = jnp.broadcast_to(w_ref[...], (length, length)).T * (1.0 / math.sqrt(length))
    cosine = weights * cos_ref[...]
    sine = weights * sin_ref[...]
    matrix = jnp.concatenate(
        [jnp.concatenate([cosine, -sine], axis=1), jnp.concatenate([sine, cosine], axis=1)], axis=0
    )
    high = matrix.astype(jnp.bfloat16)
    low = (matrix - high.astype(jnp.float32)).astype(jnp.bfloat16)

    xf[...] = x_ref[...].astype(jnp.float32)
    for th in range(spec // ch_out):
        parts = []
        for t in range(th * ch_out, (th + 1) * ch_out):
            re = xf[pl.ds(2 * t, rows, stride=2 * spec), :]
            im = xf[pl.ds(2 * t + 1, rows, stride=2 * spec), :]
            parts.append(jnp.concatenate([re, im], axis=1).astype(jnp.bfloat16))
        flat = jnp.concatenate(parts, axis=0)
        spectra = jnp.dot(flat, high, preferred_element_type=jnp.float32) + jnp.dot(
            flat, low, preferred_element_type=jnp.float32
        )
        for p in range(2):
            blocks = [
                spectra[i * rows : (i + 1) * rows, p * LANES : (p + 1) * LANES]
                for i in range(ch_out)
            ]
            blocks = swap_blocks(blocks, AVG)
            for k in range(ch_out):
                start = p * half + th * LANES
                send1[k, :, start : start + LANES] = blocks[k].astype(jnp.bfloat16)

    pl.semaphore_wait(barrier, total - 1)

    def first_copy(off, mine):
        d = lax.rem(me + off, ns)
        return pltpu.make_async_remote_copy(
            src_ref=send1.at[d // spread],
            dst_ref=held.at[mine],
            send_sem=ssem1.at[off],
            recv_sem=rsem1.at[mine],
            device_id=(b, d),
            device_id_type=MESH,
        )

    offsets = sorted(range(1, ns), key=lambda o: abs(o - ns / 2))
    for off in offsets:
        first_copy(off, me).start()
    held[me] = send1[me // spread]

    def find_dev(g, carry):
        def body(s, acc):
            return jnp.where(god_ref[s] == g, s, acc)

        dev_of[g] = lax.fori_loop(0, ns, body, jnp.int32(0), unroll=min(ns, 8))
        return carry

    lax.fori_loop(0, ns, find_dev, 0)
    quarter = lax.rem(me, spread)

    def find_col(i, carry):
        g1 = quarter * ch_out + i // ns
        o = lax.rem(i, ns)

        def body(g2, acc):
            return jnp.where(own_ref[g1, g2] == o, dev_of[g2], acc)

        table[i] = lax.fori_loop(0, ns, body, jnp.int32(0), unroll=min(ns, 8))
        return carry

    lax.fori_loop(0, ch_out * ns, find_col, 0)

    for off in offsets:
        first_copy(off, lax.rem(me + ns - off, ns)).wait_recv()

    span = ch_out * rows
    for g in range(ch_out):
        x = held[dev_of[quarter * ch_out + g]]
        left[g * rows : (g + 1) * rows, :] = x
        left[span + g * rows : span + (g + 1) * rows, :half] = x[:, half:]
        left[span + g * rows : span + (g + 1) * rows, half:] = -x[:, :half]
    per_tile = LANES // rows
    lhs = left[...]
    for h in range(ns // per_tile):
        rhs = held[h * per_tile : (h + 1) * per_tile].reshape(LANES, 2 * half)
        block = lax.dot_general(
            lhs, rhs, (((1,), (1,)), ((), ())), preferred_element_type=jnp.float32
        )
        vis[h] = block * (1.0 / (AVG * spec))
    sub = rows // per_tile
    for h in range(ns // per_tile):
        blocks = [
            vis[h, pl.ds(q, 2 * span // per_tile, stride=per_tile), :] for q in range(per_tile)
        ]
        blocks = swap_blocks(blocks, rows)
        for s in range(per_tile):
            tiles[h * per_tile + s] = blocks[s].reshape(2 * ch_out, sub, LANES)

    def build(o, carry):
        for fl in range(fl_count):
            for g in range(rpf):
                row = fl * rpf + g
                source = table[row * ns + o]
                for p in range(2):
                    mixed[fl * ns + o, p, pl.ds(g, sub, stride=rpf), :] = tiles[
                        source, p * ch_out + row
                    ]
        return carry

    lax.fori_loop(0, ns, build, 0)

    def convert(i, carry):
        send2[i] = mixed[i].astype(jnp.bfloat16)
        return carry

    lax.fori_loop(0, fl_count * ns, convert, 0)

    channel = b * ch_out + me // spread

    def target(i):
        f = quarter * fl_count + lax.rem(b + i // ns, fl_count)
        o = lax.rem(me + i, ns)
        return f, o

    def second_copy(i):
        f, o = target(i)
        return pltpu.make_async_remote_copy(
            src_ref=send2.at[lax.rem(f, fl_count) * ns + o],
            dst_ref=out_ref.at[channel],
            send_sem=ssem2.at[i],
            recv_sem=rsem2.at[channel],
            device_id=(f, o),
            device_id_type=MESH,
        )

    own_here = quarter == b // fl_count

    def start_second(i, carry):
        second_copy(i).start()
        return carry

    def wait_second(i, carry):
        second_copy(i).wait_send()
        return carry

    pl.when(jnp.logical_not(own_here))(lambda: second_copy(0).start())
    lax.fori_loop(1, fl_count * ns, start_second, 0)

    @pl.when(own_here)
    def _():
        out_ref[channel] = send2[lax.rem(b, fl_count) * ns + me]

    for off in offsets:
        first_copy(off, me).wait_send()

    def arrived(slot):
        pltpu.make_async_remote_copy(
            src_ref=send2.at[0],
            dst_ref=out_ref.at[slot],
            send_sem=ssem2.at[0],
            recv_sem=rsem2.at[slot],
            device_id=(b, me),
            device_id_type=MESH,
        ).wait_recv()

    def wait_arrival(i, carry):
        arrived(lax.rem(channel + i, nf * ch_out))
        return carry

    pl.when(jnp.logical_not(own_here))(lambda: arrived(channel))
    lax.fori_loop(1, nf * ch_out, wait_arrival, 0)
    pl.when(jnp.logical_not(own_here))(lambda: second_copy(0).wait_send())
    lax.fori_loop(1, fl_count * ns, wait_second, 0)


def shards(nf, ns, samples, window, group_of_device, owner_map):
    _, rows, spec, _, length = samples.shape
    ch_out = length // AVG
    rpf = ns // nf
    fl_count = ch_out // rpf
    per_tile = LANES // rows
    sub = rows // per_tile
    depth = 2 * spec * AVG
    index = np.arange(length)
    theta = (index[:, None] * index[None, :] % length) * (2.0 * math.pi / length)
    cosine = jnp.asarray(np.cos(theta), jnp.float32)
    sine = jnp.asarray(np.sin(theta), jnp.float32)
    x = samples.reshape(rows * spec * 2, length)
    vmem = pl.BlockSpec(memory_space=pltpu.VMEM)
    smem = pl.BlockSpec(memory_space=pltpu.SMEM)
    out = pl.pallas_call(
        functools.partial(kernel, nf, ns, rows, spec),
        out_shape=jax.ShapeDtypeStruct((nf * ch_out, 2, sub * rpf, LANES), jnp.bfloat16),
        in_specs=[vmem, vmem, vmem, vmem, smem, smem],
        out_specs=vmem,
        scratch_shapes=[
            pltpu.VMEM((rows * spec * 2, length), jnp.float32),
            pltpu.VMEM((ch_out, rows, depth), jnp.bfloat16),
            pltpu.VMEM((ns, rows, depth), jnp.bfloat16),
            pltpu.VMEM((2 * ch_out * rows, depth), jnp.bfloat16),
            pltpu.VMEM((ns // per_tile, 2 * ch_out * rows, LANES), jnp.float32),
            pltpu.VMEM((ns, 2 * ch_out, sub, LANES), jnp.float32),
            pltpu.VMEM((fl_count * ns, 2, sub * rpf, LANES), jnp.float32),
            pltpu.VMEM((fl_count * ns, 2, sub * rpf, LANES), jnp.bfloat16),
            pltpu.SMEM((ns,), jnp.int32),
            pltpu.SMEM((ch_out * ns,), jnp.int32),
            pltpu.SemaphoreType.DMA((ns,)),
            pltpu.SemaphoreType.DMA((ns,)),
            pltpu.SemaphoreType.DMA((fl_count * ns,)),
            pltpu.SemaphoreType.DMA((nf * ch_out,)),
        ],
        compiler_params=pltpu.CompilerParams(collective_id=0, has_side_effects=True),
    )(x, window.reshape(1, length), cosine, sine, group_of_device, owner_map)
    out = out.reshape(nf * ch_out, 2, sub, rpf, LANES).transpose(1, 0, 3, 2, 4)
    return out.reshape(2, nf * ch_out, 1, rpf, rows * rows)


def solution(mesh):
    return jax.shard_map(
        functools.partial(shards, mesh.shape["freq"], mesh.shape["stn"]),
        mesh=mesh,
        in_specs=(P("freq", "stn", None, None, None), P(), P(), P()),
        out_specs=P(None, None, "stn", "freq", None),
        check_vma=False,
    )
```

time: 58.4 us -> 29.1 us (0.50)
  Pallas kernels: 0 us -> 27.2 us
  local copies, waits for them, and re-layouts: 21.1 us -> 1.75 us
  waiting for transfers between devices: 13.8 us -> 0 us
  starting transfers between devices: 10.9 us -> 0 us
  blocking collectives: 8.59 us -> 0 us
  matrix products: 2.02 us -> 0 us
  other arithmetic: 1.33 us -> 0 us
    pallas_call x0 -> x1, Pallas kernels: none -> 27.2 us  [shards(): pl.pallas_call(functools.partial(kernel, nf, ns, rows, spec), out_shape=j...]
    all_to_all x2 -> x0, waiting for transfers between devices: 13.8 us -> none  [the longest x1 8.8 us: channel_plan(): lax.all_to_all(outgoing, 'stn', split_axis=2, concat_axis=2, tiled=True)]
    all_to_all x2 -> x0, starting transfers between devices: 10.9 us -> none  [the longest x1 7.28 us: channel_plan(): lax.all_to_all(copies, 'stn', split_axis=0, concat_axis=1, tiled=True)]
    all_to_all x1 -> x0, blocking collectives: 8.59 us -> none  [shards(): lax.all_to_all(by_group, 'freq', split_axis=2, concat_axis=1, tiled=True)]
    gather x10 -> x0, local copies, waits for them, and re-layouts: 4.83 us -> none  [the longest x4 2.13 us: channel_plan(): jnp.take_along_axis(vis, column_device[None, :, :, None, None], axis=2)]
    scatter x2 -> x0, local copies, waits for them, and re-layouts: 4.05 us -> none  [the longest x1 3.45 us: channel_plan(): column_for = jnp.zeros((groups, groups), jnp.int32).at[order[:, None], ow...]
    reshape x3 -> x1, local copies, waits for them, and re-layouts: 4.75 us -> 0.77 us  [shards(): return out.reshape(2, nf * ch_out, 1, rpf, rows * rows)]
    another operation x2 -> x0, local copies, waits for them, and re-layouts: 2.35 us -> none  [the longest x1 2.35 us: channel_plan(): copies = jnp.repeat(local, spread, axis=0)]
  transfers between devices with their start and end apart: 2 -> 0, of which waited for: 2 -> 0; matrix products, arithmetic and copies ran while one was open for 11% -> 0% of each run, Pallas kernels for 0% -> 0%
where the time goes in v1:
time: 29.1 us; the launch traced here: 28.9 us
  Pallas kernels  27.2 us (93%)
  local copies, waits for them, and re-layouts  1.75 us (6%)
    pallas_call x1, Pallas kernels, shards(): pl.pallas_call(functools.partial(kernel, nf, ns, rows, spec), out_shape=j...  27.2 us
    transpose x1, local copies, waits for them, and re-layouts, shards(): out = out.reshape(nf * ch_out, 2, sub, rpf, LANES).transpose(1, 0, 3, 2, 4)  0.99 us
    reshape x1, local copies, waits for them, and re-layouts, shards(): return out.reshape(2, nf * ch_out, 1, rpf, rows * rows)  0.77 us

profile of v1, /device:TPU:0, one launch (start us, length us, event | category | flops | bytes accessed | tf_op | source)
XLA Modules:
  0.0 28.9 jit_solution(16747576059620306666)
XLA Ops:
  0.0 27.2 %shard_map.64 = bf16[32,2,16,128]{3,2,1,0:T(8,128)(2,1)} custom-call(bf16[1536,128]{1,0:T(8,128)(2,1)} %bitcast.8, f32[1,128]{1,0:T(1,128)} %bitcast.9, f32[128,128]{1,0:T(8,128)} %constant.4.clone.cos_ref, f32[128,128]{1,0:T(8,128)} %constant.5.clone.sin_ref, s32[8]{0:T(128)} %god_ref.1, s32[8,8]{1,0:T(8,128)} %own_ref.1), custom_call_target="tpu_custom_call" | custom-call | tf_op jit(solution)/shard_map/pallas_call | solution.py:251
  27.2 1.0 %copy.7 = bf16[2,32,2,8,128]{4,3,2,1,0:T(8,128)(2,1)S(1)} copy(bf16[2,32,2,8,128]{4,2,3,0,1:T(2,128)(2,1)} %bitcast.7) | data formatting | bytes 524288 | tf_op jit(solution)/shard_map/transpose | solution.py:274
  28.2 0.8 %reshape.15 = bf16[2,32,1,2,1024]{4,3,2,1,0:T(2,128)(2,1)} reshape(bf16[2,32,2,8,128]{4,3,2,1,0:T(8,128)(2,1)S(1)} %copy.7) | data formatting | bytes 524288 | tf_op jit(solution)/shard_map/reshape | solution.py:275

commit v2 on v1

v2 whole, which is shorter than its diff:
```python
import functools
import math

import jax
import jax.numpy as jnp
import numpy as np
from jax import lax
from jax.experimental import pallas as pl
from jax.experimental.pallas import tpu as pltpu
from jax.sharding import PartitionSpec as P

AVG = 16
LANES = 128
MESH = pl.DeviceIdType.MESH
OUT_SPACE = pl.ANY


def swap_blocks(blocks, width):
    blocks = list(blocks)
    count = len(blocks)
    lane = lax.broadcasted_iota(jnp.int32, blocks[0].shape, 1) // width
    step = count // 2
    while step:
        upper = (lane // step) % 2 == 1
        for i in range(count):
            if (i // step) % 2 == 0:
                u, v = blocks[i], blocks[i + step]
                shift = step * width
                blocks[i] = jnp.where(upper, pltpu.roll(v, shift, 1), u)
                blocks[i + step] = jnp.where(upper, v, pltpu.roll(u, LANES - shift, 1))
        step //= 2
    return blocks


def kernel(
    nf, ns, rows, spec,
    x_hbm, w_hbm, trig_hbm, god_hbm, own_hbm,
    out_ref,
    x_ref, w_ref, trig_ref, god_ref, own_ref,
    xf, send1, held, left, vis, tiles, mixed, send2, dev_of, table,
    lsem, row_sem, ssem1, rsem1, ssem2, rsem2,
):
    length = LANES
    ch_out = length // AVG
    spread = ns // ch_out
    rpf = ns // nf
    fl_count = ch_out // rpf
    half = spec * AVG
    b = lax.axis_index("freq")
    me = lax.axis_index("stn")

    loads = [
        pltpu.make_async_copy(src, dst, lsem.at[n])
        for n, (src, dst) in enumerate(
            [
                (x_hbm, x_ref), (w_hbm, w_ref), (trig_hbm, trig_ref),
                (god_hbm, god_ref), (own_hbm, own_ref),
            ]
        )
    ]
    barrier = pltpu.get_barrier_semaphore()
    offsets = sorted(range(1, ns), key=lambda o: abs(o - ns / 2))
    for off in offsets:
        pl.semaphore_signal(
            barrier, inc=1, device_id=(b, lax.rem(me + off, ns)), device_id_type=MESH
        )
    for off in range(1, nf):
        pl.semaphore_signal(
            barrier, inc=1, device_id=(lax.rem(b + off, nf), me), device_id_type=MESH
        )
    for load in loads:
        load.start()
    for load in loads:
        load.wait()

    weights = jnp.broadcast_to(w_ref[...], (length, length)).T * (1.0 / math.sqrt(length))
    cosine = weights * trig_ref[0]
    sine = weights * trig_ref[1]
    matrix = jnp.concatenate(
        [jnp.concatenate([cosine, -sine], axis=1), jnp.concatenate([sine, cosine], axis=1)], axis=0
    )
    high = matrix.astype(jnp.bfloat16)
    low = (matrix - high.astype(jnp.float32)).astype(jnp.bfloat16)

    xf[...] = x_ref[...].astype(jnp.float32)
    for th in range(spec // ch_out):
        parts = []
        for t in range(th * ch_out, (th + 1) * ch_out):
            re = xf[pl.ds(2 * t, rows, stride=2 * spec), :]
            im = xf[pl.ds(2 * t + 1, rows, stride=2 * spec), :]
            parts.append(jnp.concatenate([re, im], axis=1).astype(jnp.bfloat16))
        flat = jnp.concatenate(parts, axis=0)
        spectra = jnp.dot(flat, high, preferred_element_type=jnp.float32) + jnp.dot(
            flat, low, preferred_element_type=jnp.float32
        )
        for p in range(2):
            blocks = [
                spectra[i * rows : (i + 1) * rows, p * LANES : (p + 1) * LANES]
                for i in range(ch_out)
            ]
            blocks = swap_blocks(blocks, AVG)
            for k in range(ch_out):
                start = p * half + th * LANES
                send1[k, :, start : start + LANES] = blocks[k].astype(jnp.bfloat16)

    pl.semaphore_wait(barrier, ns - 1 + nf - 1)

    def first_copy(off, mine):
        d = lax.rem(me + off, ns)
        return pltpu.make_async_remote_copy(
            src_ref=send1.at[d // spread],
            dst_ref=held.at[mine],
            send_sem=ssem1.at[off],
            recv_sem=rsem1.at[mine],
            device_id=(b, d),
            device_id_type=MESH,
        )

    for off in offsets:
        first_copy(off, me).start()
    for off in range(1, nf):
        pl.semaphore_signal(
            row_sem, inc=1, device_id=(lax.rem(b + off, nf), me), device_id_type=MESH
        )
    held[me] = send1[me // spread]

    def find_dev(g, carry):
        def body(s, acc):
            return jnp.where(god_ref[s] == g, s, acc)

        dev_of[g] = lax.fori_loop(0, ns, body, jnp.int32(0), unroll=min(ns, 8))
        return carry

    lax.fori_loop(0, ns, find_dev, 0)
    quarter = lax.rem(me, spread)

    def find_col(i, carry):
        g1 = quarter * ch_out + i // ns
        o = lax.rem(i, ns)

        def body(g2, acc):
            return jnp.where(own_ref[g1, g2] == o, dev_of[g2], acc)

        table[i] = lax.fori_loop(0, ns, body, jnp.int32(0), unroll=min(ns, 8))
        return carry

    lax.fori_loop(0, ch_out * ns, find_col, 0)
    pl.semaphore_wait(row_sem, nf - 1)

    for off in offsets:
        first_copy(off, lax.rem(me + ns - off, ns)).wait_recv()

    channel = b * ch_out + me // spread
    own_here = quarter == b // fl_count

    def second_copy(df, step):
        f = quarter * fl_count + lax.rem(b + df, fl_count)
        o = lax.rem(me + step, ns)
        return pltpu.make_async_remote_copy(
            src_ref=send2.at[df * ns + o],
            dst_ref=out_ref.at[:, channel],
            send_sem=ssem2.at[df * ns + step],
            recv_sem=rsem2.at[channel],
            device_id=(f, o),
            device_id_type=MESH,
        )

    per_tile = LANES // rows
    sub = rows // per_tile
    span = rpf * rows
    for df in range(fl_count):
        fl = lax.rem(b + df, fl_count)
        for g in range(rpf):
            x = held[dev_of[quarter * ch_out + fl * rpf + g]]
            left[g * rows : (g + 1) * rows, :] = x
            left[span + g * rows : span + (g + 1) * rows, :half] = x[:, half:]
            left[span + g * rows : span + (g + 1) * rows, half:] = -x[:, :half]
        lhs = left[...]
        for h in range(ns // per_tile):
            rhs = held[h * per_tile : (h + 1) * per_tile].reshape(LANES, 2 * half)
            block = lax.dot_general(
                lhs, rhs, (((1,), (1,)), ((), ())), preferred_element_type=jnp.float32
            )
            vis[h] = block * (1.0 / (AVG * spec))
            blocks = [
                vis[h, pl.ds(q, 2 * span // per_tile, stride=per_tile), :] for q in range(per_tile)
            ]
            blocks = swap_blocks(blocks, rows)
            for s in range(per_tile):
                tiles[h * per_tile + s] = blocks[s].reshape(2 * rpf, sub, LANES)

        def build(o, carry):
            for g in range(rpf):
                source = table[(fl * rpf + g) * ns + o]
                for p in range(2):
                    mixed[o, p, pl.ds(g, sub, stride=rpf), :] = tiles[source, p * rpf + g]
            for p in range(2):
                for r in range(sub):
                    send2[df * ns + o, p, :, r * LANES : (r + 1) * LANES] = mixed[
                        o, p, r * rpf : (r + 1) * rpf, :
                    ].astype(jnp.bfloat16)
            return carry

        lax.fori_loop(0, ns, build, 0, unroll=min(ns, 8))

        for off in offsets:
            second_copy(df, off).start()
        if df:
            second_copy(df, 0).start()
        else:
            pl.when(jnp.logical_not(own_here))(lambda: second_copy(0, 0).start())

    @pl.when(own_here)
    def _():
        own = pltpu.make_async_copy(send2.at[me], out_ref.at[:, channel], lsem.at[0])
        own.start()
        own.wait()

    for off in offsets:
        first_copy(off, me).wait_send()

    def arrived(slot):
        pltpu.make_async_remote_copy(
            src_ref=send2.at[0],
            dst_ref=out_ref.at[:, slot],
            send_sem=ssem2.at[0],
            recv_sem=rsem2.at[slot],
            device_id=(b, me),
            device_id_type=MESH,
        ).wait_recv()

    def wait_arrival(i, carry):
        arrived(lax.rem(channel + i, nf * ch_out))
        return carry

    pl.when(jnp.logical_not(own_here))(lambda: arrived(channel))
    lax.fori_loop(1, nf * ch_out, wait_arrival, 0)

    def wait_second(i, carry):
        second_copy(i // ns, lax.rem(i, ns)).wait_send()
        return carry

    pl.when(jnp.logical_not(own_here))(lambda: second_copy(0, 0).wait_send())
    lax.fori_loop(1, fl_count * ns, wait_second, 0)


def shards(nf, ns, samples, window, group_of_device, owner_map):
    _, rows, spec, _, length = samples.shape
    ch_out = length // AVG
    rpf = ns // nf
    fl_count = ch_out // rpf
    per_tile = LANES // rows
    sub = rows // per_tile
    depth = 2 * spec * AVG
    index = np.arange(length)
    theta = (index[:, None] * index[None, :] % length) * (2.0 * math.pi / length)
    trig = jnp.asarray(np.stack([np.cos(theta), np.sin(theta)]), jnp.float32)
    x = samples.reshape(rows * spec * 2, length)
    hbm = pl.BlockSpec(memory_space=pltpu.HBM)
    out = pl.pallas_call(
        functools.partial(kernel, nf, ns, rows, spec),
        out_shape=jax.ShapeDtypeStruct((2, nf * ch_out, rpf, sub * LANES), jnp.bfloat16),
        in_specs=[hbm] * 5,
        out_specs=pl.BlockSpec(memory_space=OUT_SPACE),
        scratch_shapes=[
            pltpu.VMEM((rows * spec * 2, length), jnp.bfloat16),
            pltpu.VMEM((1, length), jnp.float32),
            pltpu.VMEM((2, length, length), jnp.float32),
            pltpu.SMEM((ns,), jnp.int32),
            pltpu.SMEM((ns, ns), jnp.int32),
            pltpu.VMEM((rows * spec * 2, length), jnp.float32),
            pltpu.VMEM((ch_out, rows, depth), jnp.bfloat16),
            pltpu.VMEM((ns, rows, depth), jnp.bfloat16),
            pltpu.VMEM((2 * rpf * rows, depth), jnp.bfloat16),
            pltpu.VMEM((ns // per_tile, 2 * rpf * rows, LANES), jnp.float32),
            pltpu.VMEM((ns, 2 * rpf, sub, LANES), jnp.float32),
            pltpu.VMEM((ns, 2, sub * rpf, LANES), jnp.float32),
            pltpu.VMEM((fl_count * ns, 2, rpf, sub * LANES), jnp.bfloat16),
            pltpu.SMEM((ns,), jnp.int32),
            pltpu.SMEM((ch_out * ns,), jnp.int32),
            pltpu.SemaphoreType.DMA((5,)),
            pltpu.SemaphoreType.REGULAR,
            pltpu.SemaphoreType.DMA((ns,)),
            pltpu.SemaphoreType.DMA((ns,)),
            pltpu.SemaphoreType.DMA((fl_count * ns,)),
            pltpu.SemaphoreType.DMA((nf * ch_out,)),
        ],
        compiler_params=pltpu.CompilerParams(
            collective_id=0, has_side_effects=True, vmem_limit_bytes=60 * 1024 * 1024
        ),
    )(x, window.reshape(1, length), trig, group_of_device, owner_map)
    return out[:, :, None]


def solution(mesh):
    return jax.shard_map(
        functools.partial(shards, mesh.shape["freq"], mesh.shape["stn"]),
        mesh=mesh,
        in_specs=(P("freq", "stn", None, None, None), P(), P(), P()),
        out_specs=P(None, None, "stn", "freq", None),
        check_vma=False,
    )
```

time: 29.1 us -> 26.1 us (0.90)
  Pallas kernels: 27.2 us -> 24.1 us
    pallas_call x1, Pallas kernels: 27.2 us -> 24.1 us  [shards(): pl.pallas_call(functools.partial(kernel, nf, ns, rows, spec), out_shape=j...]
    unnamed x0 -> x1, local copies, waits for them, and re-layouts: none -> 1.83 us
    transpose x1 -> x0, local copies, waits for them, and re-layouts: 0.99 us -> none  [shards(): out = out.reshape(nf * ch_out, 2, sub, rpf, LANES).transpose(1, 0, 3, 2, 4)]
    reshape x1 -> x0, local copies, waits for them, and re-layouts: 0.77 us -> none  [shards(): return out.reshape(2, nf * ch_out, 1, rpf, rows * rows)]
where the time goes in v2:
time: 26.1 us; the launch traced here: 26 us
  Pallas kernels  24.1 us (92%)
  local copies, waits for them, and re-layouts  1.83 us (7%)
    pallas_call x1, Pallas kernels, shards(): pl.pallas_call(functools.partial(kernel, nf, ns, rows, spec), out_shape=j...  24.1 us
    unnamed x1, local copies, waits for them, and re-layouts  1.83 us

profile of v2, /device:TPU:0, one launch (start us, length us, event | category | flops | bytes accessed | tf_op | source)
XLA Modules:
  0.0 26.0 jit_solution(17499478213076839759)
XLA Ops:
  0.0 24.1 %shard_map.55 = bf16[2,32,2,1024]{3,2,1,0:T(2,128)(2,1)} custom-call(bf16[1536,128]{1,0:T(8,128)(2,1)} %bitcast.6, f32[1,128]{1,0:T(1,128)} %bitcast.7, f32[2,128,128]{2,1,0:T(8,128)} %constant.2.clone.trig_hbm, s32[8]{0:T(128)} %god_hbm.1, s32[8,8]{1,0:T(8,128)} %own_hbm.1), custom_call_target="tpu_custom_call" | custom-call | tf_op jit(solution)/shard_map/pallas_call | solution.py:260
  24.1 1.8 %copy.8 = bf16[2,32,1,2,1024]{4,3,2,1,0:T(2,128)(2,1)} copy(bf16[2,32,1,2,1024]{4,3,2,1,0:T(2,128)(2,1)} %bitcast.5) | data formatting | bytes 524288

commit v3 on v2

--- a/solution.py
+++ b/solution.py
@@ -12,7 +12,7 @@
 AVG = 16
 LANES = 128
 MESH = pl.DeviceIdType.MESH
-OUT_SPACE = pl.ANY
+OUT_SPACE = pltpu.VMEM
 
 
 def swap_blocks(blocks, width):
@@ -259,7 +259,7 @@
     hbm = pl.BlockSpec(memory_space=pltpu.HBM)
     out = pl.pallas_call(
         functools.partial(kernel, nf, ns, rows, spec),
-        out_shape=jax.ShapeDtypeStruct((2, nf * ch_out, rpf, sub * LANES), jnp.bfloat16),
+        out_shape=pltpu.VMEM((2, nf * ch_out, rpf, sub * LANES), jnp.bfloat16),
         in_specs=[hbm] * 5,
         out_specs=pl.BlockSpec(memory_space=OUT_SPACE),
         scratch_shapes=[

time: 26.1 us -> 24.8 us (0.950)
  local copies, waits for them, and re-layouts: 1.83 us -> 0.71 us
    unnamed x1, local copies, waits for them, and re-layouts: 1.83 us -> 0.71 us
where the time goes in v3:
time: 24.8 us; the launch traced here: 24.7 us
  Pallas kernels  24 us (97%)
  local copies, waits for them, and re-layouts  0.71 us (3%)
    pallas_call x1, Pallas kernels, shards(): pl.pallas_call(functools.partial(kernel, nf, ns, rows, spec), out_shape=p...  24 us
    unnamed x1, local copies, waits for them, and re-layouts  0.71 us

profile of v3, /device:TPU:0, one launch (start us, length us, event | category | flops | bytes accessed | tf_op | source)
XLA Modules:
  0.0 24.7 jit_solution(145328473985035548)
XLA Ops:
  0.0 24.0 %shard_map.55 = bf16[2,32,2,1024]{3,2,1,0:T(2,128)(2,1)S(1)} custom-call(bf16[1536,128]{1,0:T(8,128)(2,1)} %bitcast.6, f32[1,128]{1,0:T(1,128)} %bitcast.7, f32[2,128,128]{2,1,0:T(8,128)} %constant.2.clone.trig_hbm, s32[8]{0:T(128)} %god_hbm.1, s32[8,8]{1,0:T(8,128)} %own_hbm.1), custom_call_target="tpu_custom_call" | custom-call | tf_op jit(solution)/shard_map/pallas_call | solution.py:260
  24.0 0.7 %copy.8 = bf16[2,32,1,2,1024]{4,3,2,1,0:T(2,128)(2,1)} copy(bf16[2,32,1,2,1024]{4,3,2,1,0:T(2,128)(2,1)S(1)} %bitcast.5) | data formatting | bytes 524288

commit v4 on v3

--- a/solution.py
+++ b/solution.py
@@ -154,7 +154,7 @@
     own_here = quarter == b // fl_count
 
     def second_copy(df, step):
-        f = quarter * fl_count + lax.rem(b + df, fl_count)
+        f = quarter * fl_count + lax.rem(b + df + 1, fl_count)
         o = lax.rem(me + step, ns)
         return pltpu.make_async_remote_copy(
             src_ref=send2.at[df * ns + o],
@@ -169,7 +169,7 @@
     sub = rows // per_tile
     span = rpf * rows
     for df in range(fl_count):
-        fl = lax.rem(b + df, fl_count)
+        fl = lax.rem(b + df + 1, fl_count)
         for g in range(rpf):
             x = held[dev_of[quarter * ch_out + fl * rpf + g]]
             left[g * rows : (g + 1) * rows, :] = x
@@ -203,16 +203,16 @@
 
         lax.fori_loop(0, ns, build, 0, unroll=min(ns, 8))
 
-        for off in offsets:
+        for off in reversed(offsets):
             second_copy(df, off).start()
-        if df:
+        if df != fl_count - 1:
             second_copy(df, 0).start()
         else:
-            pl.when(jnp.logical_not(own_here))(lambda: second_copy(0, 0).start())
+            pl.when(jnp.logical_not(own_here))(lambda: second_copy(fl_count - 1, 0).start())
 
     @pl.when(own_here)
     def _():
-        own = pltpu.make_async_copy(send2.at[me], out_ref.at[:, channel], lsem.at[0])
+        own = pltpu.make_async_copy(send2.at[(fl_count - 1) * ns + me], out_ref.at[:, channel], lsem.at[0])
         own.start()
         own.wait()
 
@@ -240,8 +240,9 @@
         second_copy(i // ns, lax.rem(i, ns)).wait_send()
         return carry
 
-    pl.when(jnp.logical_not(own_here))(lambda: second_copy(0, 0).wait_send())
-    lax.fori_loop(1, fl_count * ns, wait_second, 0)
+    pl.when(jnp.logical_not(own_here))(lambda: second_copy(fl_count - 1, 0).wait_send())
+    lax.fori_loop(0, (fl_count - 1) * ns, wait_second, 0)
+    lax.fori_loop((fl_count - 1) * ns + 1, fl_count * ns, wait_second, 0)
 
 
 def shards(nf, ns, samples, window, group_of_device, owner_map):

time: 24.8 us -> 24.3 us (0.980)
  Pallas kernels: 24 us -> 23.5 us
    pallas_call x1, Pallas kernels: 24 us -> 23.5 us  [shards(): pl.pallas_call(functools.partial(kernel, nf, ns, rows, spec), out_shape=p...]
where the time goes in v4:
time: 24.3 us; the launch traced here: 24.2 us
  Pallas kernels  23.5 us (97%)
  local copies, waits for them, and re-layouts  0.71 us (3%)
    pallas_call x1, Pallas kernels, shards(): pl.pallas_call(functools.partial(kernel, nf, ns, rows, spec), out_shape=p...  23.5 us
    unnamed x1, local copies, waits for them, and re-layouts  0.71 us

profile of v4, /device:TPU:0, one launch (start us, length us, event | category | flops | bytes accessed | tf_op | source)
XLA Modules:
  0.0 24.2 jit_solution(875831361150207061)
XLA Ops:
  0.0 23.5 %shard_map.55 = bf16[2,32,2,1024]{3,2,1,0:T(2,128)(2,1)S(1)} custom-call(bf16[1536,128]{1,0:T(8,128)(2,1)} %bitcast.6, f32[1,128]{1,0:T(1,128)} %bitcast.7, f32[2,128,128]{2,1,0:T(8,128)} %constant.2.clone.trig_hbm, s32[8]{0:T(128)} %god_hbm.1, s32[8,8]{1,0:T(8,128)} %own_hbm.1), custom_call_target="tpu_custom_call" | custom-call | tf_op jit(solution)/shard_map/pallas_call | solution.py:261
  23.5 0.7 %copy.8 = bf16[2,32,1,2,1024]{4,3,2,1,0:T(2,128)(2,1)} copy(bf16[2,32,1,2,1024]{4,3,2,1,0:T(2,128)(2,1)S(1)} %bitcast.5) | data formatting | bytes 524288
